TPU v7x, 128 devices: a whole 4x4x4 slice. The times are simulated.
128 devices in a mesh: grp: 4 (over x), tile: 32 (over y, z, core).
Axes of the slice: x: 4, y: 4, z: 4, core: 2. Of those that a mesh axis runs over, the one named last changes fastest.
Arguments:
- descriptors: bfloat16 [64, 4096, 256], P('grp', 'tile'), may hold values from -8 to 8
- pairs: int32 [32, 2], P('grp'), may hold values from 0 to 63, as said below
- counts: int32 [64], replicated, may hold values from 1024 to 4096
Outputs:
- row_lse: float32 [32, 4096], P('grp', 'tile')
- col_lse: float32 [32, 4096], P('grp', 'tile')
- best_log: float32 [32, 4096], P('grp', 'tile')
Inputs may be any that keep to these rules, and one draw needn't show every extreme that they name: `pairs`: the two images of a pair differ.
All inputs are finite; a program needn't handle non-finite values.
Results may differ from a plain program's by a relative error of at most 0.0003.
Values may be sent and summed in bfloat16 or wider, within the bound.
A program may use at most 64 MiB of HBM per device.

v0:
```python
import math
import jax
import jax.numpy as jnp
from jax import lax
from jax.sharding import Mesh
from jax.sharding import PartitionSpec as P

QBLK = 4
TILE = ("tile_0", "tile_1", "tile_2")
NEGATIVE = -1e30


def in_one_piece(arrays, axis, split_dim, concat_dim, along):
    both = jnp.concatenate(arrays, axis=along)
    out, at, outs = (
        lax.all_to_all(both, axis, split_axis=split_dim, concat_axis=concat_dim, tiled=True),
        0,
        [],
    )
    for a in arrays:
        outs.append(lax.slice_in_dim(out, at, at + a.shape[along], axis=along))
        at += a.shape[along]
    return tuple(outs)


def in_blocks(value, dim, count):
    lengths = value.shape
    tiles = value.reshape(*lengths[:dim], count, lengths[dim] // count, *lengths[dim + 1 :])
    return jnp.moveaxis(tiles, dim, 0)


def joined_along(tiles, dim):
    lengths = list(tiles.shape[1:])
    lengths[dim] *= tiles.shape[0]
    return jnp.moveaxis(tiles, 0, dim).reshape(lengths)


def exchange_in_order(tiles, axes, turns):
    inside = tiles.shape[1:]
    out = tiles.reshape(*(lax.axis_size(a) for a in axes), *inside)
    for k in turns:
        out = lax.all_to_all(out, axes[k], k, k, tiled=True)
    return out.reshape(-1, *inside)


def core_and_chips(value, groups, turns, split_dim, concat_dim):
    count = lax.axis_size(groups[0]) * lax.axis_size(groups[1])
    tiles = in_blocks(value, split_dim, count)
    return joined_along(exchange_in_order(tiles, groups, turns), concat_dim)


def join_stats(earlier, later):
    highest = jnp.maximum(earlier[0], later[0])
    summed = earlier[1] * jnp.exp(earlier[0] - highest) + later[1] * jnp.exp(later[0] - highest)
    return (highest, summed)


def slot_first(item, query_index, score_scale):
    query_rows, key_image, query_count, key_count = item
    height = query_rows.shape[0]
    width = query_rows.shape[1]
    total_keys = key_image.shape[0]
    block = min(512, height)
    number = height // block
    key_mask = (lax.iota(jnp.int32, total_keys) < key_count)[None, :]
    grouped = query_rows.reshape(number, block, width)
    index_groups = query_index.reshape(number, block)

    def first_pass(carried, inputs):
        block_rows, block_index = inputs
        scores = (
            jnp.einsum("qd,kd->qk", block_rows, key_image, preferred_element_type=jnp.float32)
            * score_scale
        )
        query_mask = (block_index < query_count)[:, None]
        row_top = jnp.max(jnp.where(key_mask, scores, NEGATIVE), axis=1)
        row_total = jnp.sum(jnp.where(key_mask, jnp.exp(scores - row_top[:, None]), 0.0), axis=1)
        col_top = jnp.max(jnp.where(query_mask, scores, NEGATIVE), axis=0)
        col_total = jnp.sum(jnp.where(query_mask, jnp.exp(scores - col_top[None, :]), 0.0), axis=0)
        return (join_stats(carried, (col_top, col_total)), row_top + jnp.log(row_total))

    start_stats = (
        jnp.full((total_keys,), NEGATIVE, jnp.float32),
        jnp.zeros((total_keys,), jnp.float32),
    )
    col_stats, row_values = lax.scan(first_pass, start_stats, (grouped, index_groups))
    return (col_stats[0], col_stats[1], row_values.reshape(height))


def slot_second(item, query_index, score_scale):
    query_rows, key_image, row_values, col_values, query_count, key_count = item
    height = query_rows.shape[0]
    width = query_rows.shape[1]
    total_keys = key_image.shape[0]
    block = min(512, height)
    number = height // block
    key_mask = (lax.iota(jnp.int32, total_keys) < key_count)[None, :]
    grouped = query_rows.reshape(number, block, width)
    lse_groups = row_values.reshape(number, block)

    def second_pass(carried, inputs):
        block_rows, block_lse = inputs
        scores = (
            jnp.einsum("qd,kd->qk", block_rows, key_image, preferred_element_type=jnp.float32)
            * score_scale
        )
        best = (
            jnp.max(jnp.where(key_mask, 2.0 * scores - col_values[None, :], NEGATIVE), axis=1)
            - block_lse
        )
        return (carried, best)

    unused, best_values = lax.scan(second_pass, jnp.int32(0), (grouped, lse_groups))
    query_valid = query_index < query_count
    return (
        jnp.where(query_valid, row_values, 0.0),
        jnp.where(query_valid, best_values.reshape(height), 0.0),
    )


def paired_blocks(queries, keys_local, query_counts, key_counts, score_scale):
    devices_here = lax.axis_size(TILE)
    rows = queries.shape[1]
    width = queries.shape[2]
    slots = devices_here // QBLK
    sub = rows // QBLK
    pair_count = queries.shape[0]
    per_slot = -(-pair_count // slots)
    padded = per_slot * slots
    query_send = (
        queries.reshape(slots, per_slot, QBLK, sub, width)
        .transpose(0, 2, 1, 3, 4)
        .reshape(devices_here, per_slot, sub, width)
    )
    key_send = jnp.broadcast_to(
        keys_local.reshape(slots, 1, per_slot, rows, width), (slots, QBLK, per_slot, rows, width)
    ).reshape(devices_here, per_slot, rows, width)
    query_got, key_got = in_one_piece((query_send, key_send), TILE, 0, 0, 2)
    query_here = query_got.transpose(1, 0, 2, 3).reshape(per_slot, devices_here * sub, width)
    key_here = key_got.transpose(1, 0, 2, 3).reshape(per_slot, devices_here * rows, width)
    place = lax.axis_index(TILE)
    slot = place // QBLK
    quarter = place % QBLK
    query_index = (
        lax.iota(jnp.int32, devices_here)[:, None] * rows
        + quarter * sub
        + lax.iota(jnp.int32, sub)[None, :]
    ).reshape(devices_here * sub)
    query_own = lax.dynamic_slice_in_dim(query_counts, slot * per_slot, per_slot, 0)
    key_own = lax.dynamic_slice_in_dim(key_counts, slot * per_slot, per_slot, 0)
    col_top, col_total, row_values = lax.map(
        lambda item: slot_first(item, query_index, score_scale),
        (query_here, key_here, query_own, key_own),
    )

    def by_block(values):
        return values.reshape(per_slot, devices_here, rows).transpose(1, 0, 2)

    top_got, total_got = in_one_piece((by_block(col_top), by_block(col_total)), TILE, 0, 0, 1)
    top_got = top_got.reshape(slots, QBLK, per_slot, rows)
    total_got = total_got.reshape(slots, QBLK, per_slot, rows)
    stats = (top_got[:, 0], total_got[:, 0])
    for member in range(1, QBLK):
        stats = join_stats(stats, (top_got[:, member], total_got[:, member]))
    col_block = stats[0] + jnp.log(stats[1])
    col_send = jnp.broadcast_to(col_block[:, None], (slots, QBLK, per_slot, rows)).reshape(
        devices_here, per_slot, rows
    )
    col_got = core_and_chips(col_send, (("tile_0", "tile_1"), "tile_2"), (1, 0), 0, 0)
    col_values = col_got.transpose(1, 0, 2).reshape(per_slot, devices_here * rows)
    row_out, best_out = lax.map(
        lambda item: slot_second(item, query_index, score_scale),
        (query_here, key_here, row_values, col_values, query_own, key_own),
    )

    def to_owner(values):
        return values.reshape(per_slot, devices_here, sub).transpose(1, 0, 2)

    row_got, best_got = (
        lax.all_to_all(to_owner(row_out), TILE, split_axis=0, concat_axis=0, tiled=True),
        lax.all_to_all(to_owner(best_out), TILE, split_axis=0, concat_axis=0, tiled=True),
    )

    def from_slots(values):
        return (
            values.reshape(slots, QBLK, per_slot, sub).transpose(0, 2, 1, 3).reshape(padded, rows)
        )

    key_place = place * rows + lax.iota(jnp.int32, rows)
    key_valid_own = key_place[None, :] < key_counts[:, None]
    col_out = jnp.where(key_valid_own, col_block.reshape(padded, rows), 0.0)
    return (from_slots(row_got), col_out, from_slots(best_got))


def local(descriptors, pairs, counts):
    score_scale = 2.0 / math.sqrt(descriptors.shape[2])
    image_rows = lax.all_gather(descriptors, "grp", axis=0, tiled=True)
    image_ids = lax.iota(jnp.int32, counts.shape[0])
    first_image = pairs[:, 0]
    second = pairs[:, 1]
    query_counts = jnp.sum(
        jnp.where(first_image[:, None] == image_ids[None, :], counts[None, :], 0), axis=1
    )
    key_counts = jnp.sum(
        jnp.where(second[:, None] == image_ids[None, :], counts[None, :], 0), axis=1
    )
    queries = jnp.take(image_rows, first_image, axis=0)
    keys_local = jnp.take(image_rows, second, axis=0)
    return paired_blocks(queries, keys_local, query_counts, key_counts, score_scale)


def solution(mesh):
    torus = Mesh(
        mesh.devices.reshape(mesh.shape["grp"], 4, 4, 2), ("grp", "tile_0", "tile_1", "tile_2")
    )
    return jax.shard_map(
        local,
        mesh=torus,
        in_specs=(P("grp", TILE, None), P("grp", None), P()),
        out_specs=(P("grp", TILE), P("grp", TILE), P("grp", TILE)),
        check_vma=False,
    )
```

profile of v0, /device:TPU:1, one launch (start us, length us, event | category | flops | bytes accessed | tf_op | source)
XLA Modules:
  0.0 198.5 jit_solution(10425971025592148428)
XLA Ops:
  7.2 0.0 all-gather.2.cloned.1.call-start
  7.2 0.7 all-gather.2.cloned.1.call-update
  7.9 0.8 compare_and_fusion.1
  8.7 52.2 %all-gather.2.cloned.1.call-done = bf16[64,128,256]{2,1,0:T(8,128)(2,1)} async-done(((bf16[16,128,256]{2,1,0:T(8,128)(2,1)}), bf16[64,128,256]{2,1,0:T(8,128)(2,1)}) %all-gather.2.cloned.1.call-update) | async-done | bytes 4194320 | tf_op jit(solution)/shard_map/all_gather | solution.py:197
  60.9 2.8 %gather_fusion = bf16[8,128,256]{2,1,0:T(8,128)(2,1)S(1)} fusion(bf16[64,128,256]{2,1,0:T(8,128)(2,1)} %all-gather.2.cloned.1.call-done, s32[1024]{0:T(1024)S(1)} %pad_clamp_fusion.1), kind=kCustom, calls=%fused_computation.clone | custom fusion | bytes 1048608 | tf_op jit(solution)/shard_map/jit(_take)/gather | solution.py:207
  63.6 0.0 copy-start
  63.7 0.0 copy-start.1
  63.7 2.8 %gather_fusion.1 = bf16[8,128,256]{2,1,0:T(8,128)(2,1)S(1)} fusion(bf16[64,128,256]{2,1,0:T(8,128)(2,1)} %all-gather.2.cloned.1.call-done, s32[1024]{0:T(1024)S(1)} %pad_clamp_fusion), kind=kCustom, calls=%fused_computation.1.clone | custom fusion | bytes 1048608 | tf_op jit(solution)/shard_map/jit(_take)/gather | solution.py:208
  66.5 0.2 broadcast_select_fusion
  66.6 0.2 broadcast_in_dim.140
  66.9 1.7 pad_maximum_fusion
  68.6 7.9 %all-to-all-start = ((bf16[32,1,160,256]{3,2,1,0:T(8,128)(2,1)}), bf16[32,1,160,256]{3,2,1,0:T(8,128)(2,1)S(1)}, u32[]{:S(2)}, u32[]{:S(2)}) async-start(bf16[32,1,160,256]{3,2,1,0:T(8,128)(2,1)} %pad_maximum_fusion), calls=%async_computation | async-start | bytes 5242880 | tf_op jit(solution)/shard_map/all_to_all | solution.py:16
  76.5 0.0 copy-done
  76.5 0.0 copy-done.1
  76.5 0.2 select_reduce_fusion.5
  76.8 0.6 dynamic_slice.52
  77.4 0.6 dynamic_slice.53
  77.9 0.1 add.159
  78.0 0.1 add.160
  78.1 0.1 add.162
  78.2 32.2 %all-to-all-done = bf16[32,1,160,256]{3,2,1,0:T(8,128)(2,1)S(1)} async-done(((bf16[32,1,160,256]{3,2,1,0:T(8,128)(2,1)}), bf16[32,1,160,256]{3,2,1,0:T(8,128)(2,1)S(1)}, u32[]{:S(2)}, u32[]{:S(2)}) %all-to-all-start) | async-done | bytes 2621472 | tf_op jit(solution)/shard_map/all_to_all | solution.py:16
  110.4 1.5 slice.61
  112.0 20.6 %while.48 = (s32[]{:T(128)}, f32[4096]{0:T(1024)S(1)}, f32[4096]{0:T(1024)S(1)}, f32[2,512]{1,0:T(2,128)S(1)}, s32[2,512]{1,0:T(2,128)S(1)}, /*index=5*/s32[]{:T...) while((s32[]{:T(128)}, f32[4096]{0:T(1024)S(1)}, ...), condition=%wide.region_7.9_spmd.clone, body=%wide.region_2.8_spmd.clone.sunk | while | flops 1098936320 | bytes 19316360 | solution.py:86
  112.0 0.7 compare_reduce_fusion.8
  112.6 0.7 compare_reduce_fusion.7
  113.3 4.0 %select_reduce_fusion.11 = (f32[512]{0:T(512)S(1)}, f32[4096]{0:T(1024)S(1)}, f32[512,4096]{1,0:T(8,128)S(1)}) fusion(pred[4096]{0:T(1024)(128)(4,1)S(1)} %compare_reduce_fusion.7, pred[512]{0:T(512)(128)(4,1)S(1)} %compare_reduce_fusion.8, bf16[4096,256]{1,0:T(8,128)(2,1)} %get-tuple-element.457, bf16[2,512,256]{2,1,0:T(8,128)(2,1)S(1)} %get-tuple-element.456, ...), kind=kOutput, calls=%fused_computation.11.clone.1 | convolution fusion | flops 1084222976 | bytes 10770948 | tf_op jit(solution)/shard_map/while/body/eval_jaxpr/while/body/eval_jaxpr/qd,kd->qk/dot_general | solution.py:72
  117.3 4.8 %select_reduce_fusion.12 = (f32[512]{0:T(512)S(1)}, f32[4096]{0:T(1024)S(1)}) fusion(f32[512,4096]{1,0:T(8,128)S(1)} %get-tuple-element.421, f32[512]{0:T(512)S(1)} %get-tuple-element.422, pred[4096]{0:T(1024)(128)(4,1)S(1)} %compare_reduce_fusion.7, f32[4096]{0:T(1024)S(1)} %get-tuple-element.423, pred[512]{0:T(512)(128)(4,1)S(1)} %compare_reduce_fusion.8), kind=kLoop, calls=%fused_computation.10.clone.1 | loop fusion | flops 14675456 | bytes 8430080 | tf_op jit(solution)/shard_map/while/body/eval_jaxpr/while/body/eval_jaxpr/reduce_sum | solution.py:77
  122.3 0.7 compare_reduce_fusion.8
  122.9 0.7 compare_reduce_fusion.7
  123.6 3.9 %select_reduce_fusion.11 = (f32[512]{0:T(512)S(1)}, f32[4096]{0:T(1024)S(1)}, f32[512,4096]{1,0:T(8,128)S(1)}) fusion(pred[4096]{0:T(1024)(128)(4,1)S(1)} %compare_reduce_fusion.7, pred[512]{0:T(512)(128)(4,1)S(1)} %compare_reduce_fusion.8, bf16[4096,256]{1,0:T(8,128)(2,1)} %get-tuple-element.457, bf16[2,512,256]{2,1,0:T(8,128)(2,1)S(1)} %get-tuple-element.456, ...), kind=kOutput, calls=%fused_computation.11.clone.1 | convolution fusion | flops 1084222976 | bytes 10770948 | tf_op jit(solution)/shard_map/while/body/eval_jaxpr/while/body/eval_jaxpr/qd,kd->qk/dot_general | solution.py:72
  127.6 4.8 %select_reduce_fusion.12 = (f32[512]{0:T(512)S(1)}, f32[4096]{0:T(1024)S(1)}) fusion(f32[512,4096]{1,0:T(8,128)S(1)} %get-tuple-element.421, f32[512]{0:T(512)S(1)} %get-tuple-element.422, pred[4096]{0:T(1024)(128)(4,1)S(1)} %compare_reduce_fusion.7, f32[4096]{0:T(1024)S(1)} %get-tuple-element.423, pred[512]{0:T(512)(128)(4,1)S(1)} %compare_reduce_fusion.8), kind=kLoop, calls=%fused_computation.10.clone.1 | loop fusion | flops 14675456 | bytes 8430080 | tf_op jit(solution)/shard_map/while/body/eval_jaxpr/while/body/eval_jaxpr/reduce_sum | solution.py:77
  132.6 11.1 %all_to_all.30 = f32[32,2,128]{2,1,0:T(2,128)S(1)} all-to-all(f32[32,2,128]{2,1,0:T(2,128)S(1)} %pad_maximum_fusion.1), channel_id=1, replica_groups=mesh['grp'=4,'tile_0'=4,'tile_1'=4,'tile_2'=2] {'tile_0','tile_1','tile_2'}, dimensions={0} | all-to-all | bytes 65536 | tf_op jit(solution)/shard_map/all_to_all | solution.py:16
  143.8 3.8 %all_to_all.31 = f32[16,2,1,1,128]{4,3,2,0,1:T(1,128)S(1)} all-to-all(f32[16,2,1,1,128]{4,3,2,0,1:T(1,128)S(1)} %broadcast_in_dim.147), channel_id=1, replica_groups=mesh['grp'=4,'tile_0'=4,'tile_1'=4,'tile_2'=2] {'tile_2'}, dimensions={1} | all-to-all | bytes 32768 | tf_op jit(solution)/shard_map/all_to_all | solution.py:42
  147.5 0.6 copy.107
  148.1 3.5 %all-to-all-start.4 = ((f32[16,2,1,1,128]{4,3,2,1,0:T(1,128)}), f32[16,2,1,1,128]{4,3,2,1,0:T(1,128)S(1)}, u32[]{:S(2)}, u32[]{:S(2)}) async-start(f32[16,2,1,1,128]{4,3,2,1,0:T(1,128)} %copy.107), calls=%async_computation.4 | async-start | bytes 32768 | tf_op jit(solution)/shard_map/all_to_all | solution.py:42
  151.7 0.1 squeeze.81
  151.8 6.3 %all-to-all-done.4 = f32[16,2,1,1,128]{4,3,2,1,0:T(1,128)S(1)} async-done(((f32[16,2,1,1,128]{4,3,2,1,0:T(1,128)}), f32[16,2,1,1,128]{4,3,2,1,0:T(1,128)S(1)}, u32[]{:S(2)}, u32[]{:S(2)}) %all-to-all-start.4) | async-done | bytes 16416 | tf_op jit(solution)/shard_map/all_to_all | solution.py:42
  158.0 7.6 %while.47 = (s32[]{:T(128)}, f32[2,512]{1,0:T(2,128)S(1)}, bf16[2,512,256]{2,1,0:T(8,128)(2,1)S(1)}, bf16[4096,256]{1,0:T(8,128)(2,1)}, f32[4096]{0:T(1024)S(1)}...) while((s32[]{:T(128)}, f32[2,512]{1,0:T(2,128)S(1)}, ...), condition=%wide.region_10.12_spmd.clone, body=%wide.region_8.11_spmd.clone.sunk | while | flops 1082134528 | bytes 2396269 | solution.py:113
  158.0 0.7 compare_reduce_fusion.6
  158.7 3.0 %select_reduce_fusion.10 = f32[512]{0:T(512)S(1)} fusion(bf16[4096,256]{1,0:T(8,128)(2,1)} %get-tuple-element.482, f32[4096]{0:T(1024)S(1)} %get-tuple-element.483, pred[4096]{0:T(1024)(128)(4,1)S(1)} %compare_reduce_fusion.6, bf16[2,512,256]{2,1,0:T(8,128)(2,1)S(1)} %get-tuple-element.481, s32[]{:T(128)} %get-tuple-element.470), kind=kOutput, calls=%fused_computation.4.clone.1 | convolution fusion | flops 1082129920 | bytes 2381828 | tf_op jit(solution)/shard_map/while/body/eval_jaxpr/while/body/eval_jaxpr/qd,kd->qk/dot_general | solution.py:104
  161.8 0.7 compare_reduce_fusion.6
  162.5 3.0 %select_reduce_fusion.10 = f32[512]{0:T(512)S(1)} fusion(bf16[4096,256]{1,0:T(8,128)(2,1)} %get-tuple-element.482, f32[4096]{0:T(1024)S(1)} %get-tuple-element.483, pred[4096]{0:T(1024)(128)(4,1)S(1)} %compare_reduce_fusion.6, bf16[2,512,256]{2,1,0:T(8,128)(2,1)S(1)} %get-tuple-element.481, s32[]{:T(128)} %get-tuple-element.470), kind=kOutput, calls=%fused_computation.4.clone.1 | convolution fusion | flops 1082129920 | bytes 2381828 | tf_op jit(solution)/shard_map/while/body/eval_jaxpr/while/body/eval_jaxpr/qd,kd->qk/dot_general | solution.py:104
  165.6 0.1 reshape.246
  165.7 1.4 compare_select_fusion
  167.1 4.9 %all-to-all-start.1 = ((f32[32,1,32]{2,1,0:T(1,128)}), f32[32,1,32]{2,1,0:T(1,128)S(1)}, u32[]{:S(2)}, u32[]{:S(2)}) async-start(f32[32,1,32]{2,1,0:T(1,128)} %get-tuple-element.313), calls=%async_computation.1 | async-start | bytes 32768 | tf_op jit(solution)/shard_map/all_to_all | solution.py:180
  172.0 7.1 %all-to-all-done.1 = f32[32,1,32]{2,1,0:T(1,128)S(1)} async-done(((f32[32,1,32]{2,1,0:T(1,128)}), f32[32,1,32]{2,1,0:T(1,128)S(1)}, u32[]{:S(2)}, u32[]{:S(2)}) %all-to-all-start.1) | async-done | bytes 4128 | tf_op jit(solution)/shard_map/all_to_all | solution.py:180
  179.1 4.2 %all-to-all-start.5 = ((f32[32,1,32]{2,1,0:T(1,128)}), f32[32,1,32]{2,1,0:T(1,128)S(1)}, u32[]{:S(2)}, u32[]{:S(2)}) async-start(f32[32,1,32]{2,1,0:T(1,128)} %get-tuple-element.312), calls=%async_computation.5 | async-start | bytes 32768 | tf_op jit(solution)/shard_map/all_to_all | solution.py:181
  183.2 0.7 add_select_fusion
  183.9 0.5 broadcast.199
  184.4 0.7 reduce.12
  185.1 0.7 reshape_transpose_reshape.10
  185.8 4.5 %all-to-all-done.5 = f32[32,1,32]{2,1,0:T(1,128)S(1)} async-done(((f32[32,1,32]{2,1,0:T(1,128)}), f32[32,1,32]{2,1,0:T(1,128)S(1)}, u32[]{:S(2)}, u32[]{:S(2)}) %all-to-all-start.5) | async-done | bytes 4128 | tf_op jit(solution)/shard_map/all_to_all | solution.py:181
  190.3 0.7 reduce.13
  191.0 0.7 reshape_transpose_reshape.11
  (30 shorter events, 0.5 us)
Async XLA Ops:
  7.2 53.7 %all-gather.2.cloned.1.call-start = ((), (), s32[]{:S(2)}) async-start(), calls=%async_computation.6 | async-start | bytes 5242880 | tf_op jit(solution)/shard_map/all_gather | solution.py:197
  63.6 12.9 %copy-start = (s32[8,2]{0,1:T(2,128)S(1)}, s32[8,2]{0,1:T(2,128)}, u32[]{:S(2)}) copy-start(s32[8,2]{0,1:T(2,128)} %param.10) | copy-start | bytes 196
  63.7 12.9 %copy-start.1 = (s32[64]{0:T(128)S(1)}, s32[64]{0:T(128)}, u32[]{:S(2)}) copy-start(s32[64]{0:T(128)} %param.11) | copy-start | bytes 772
  68.6 41.8 %all-to-all-start = ((bf16[32,1,160,256]{3,2,1,0:T(8,128)(2,1)}), bf16[32,1,160,256]{3,2,1,0:T(8,128)(2,1)S(1)}, u32[]{:S(2)}, u32[]{:S(2)}) async-start(bf16[32,1,160,256]{3,2,1,0:T(8,128)(2,1)} %pad_maximum_fusion), calls=%async_computation | async-start | bytes 5242880 | tf_op jit(solution)/shard_map/all_to_all | solution.py:16
  148.1 9.9 %all-to-all-start.4 = ((f32[16,2,1,1,128]{4,3,2,1,0:T(1,128)}), f32[16,2,1,1,128]{4,3,2,1,0:T(1,128)S(1)}, u32[]{:S(2)}, u32[]{:S(2)}) async-start(f32[16,2,1,1,128]{4,3,2,1,0:T(1,128)} %copy.107), calls=%async_computation.4 | async-start | bytes 32768 | tf_op jit(solution)/shard_map/all_to_all | solution.py:42
  167.1 12.0 %all-to-all-start.1 = ((f32[32,1,32]{2,1,0:T(1,128)}), f32[32,1,32]{2,1,0:T(1,128)S(1)}, u32[]{:S(2)}, u32[]{:S(2)}) async-start(f32[32,1,32]{2,1,0:T(1,128)} %get-tuple-element.313), calls=%async_computation.1 | async-start | bytes 32768 | tf_op jit(solution)/shard_map/all_to_all | solution.py:180
  179.1 11.2 %all-to-all-start.5 = ((f32[32,1,32]{2,1,0:T(1,128)}), f32[32,1,32]{2,1,0:T(1,128)S(1)}, u32[]{:S(2)}, u32[]{:S(2)}) async-start(f32[32,1,32]{2,1,0:T(1,128)} %get-tuple-element.312), calls=%async_computation.5 | async-start | bytes 32768 | tf_op jit(solution)/shard_map/all_to_all | solution.py:181
Sparse Core Ops, SparseCore 0:
  9.6 51.1 all-gather.1
where the time goes:
time: 199 us
  waiting for transfers between devices  103 us (52%)
  starting transfers between devices  20.5 us (10%)
  other arithmetic  20.3 us (10%)
  blocking collectives  14.8 us (7%)
  between operations  14.3 us (7%)
  matrix products  13.9 us (7%)
  local copies, waits for them, and re-layouts  11.7 us (6%)
    all_gather x1, waiting for transfers between devices, local(): image_rows = lax.all_gather(descriptors, 'grp', axis=0, tiled=True)  52.2 us
    all_to_all x1, waiting for transfers between devices, in_one_piece(): lax.all_to_all(both, axis, split_axis=split_dim, concat_axis=concat_dim,...  32.2 us
    all_to_all x1, blocking collectives, in_one_piece(): lax.all_to_all(both, axis, split_axis=split_dim, concat_axis=concat_dim,...  11.1 us
    reduce_sum x2, other arithmetic, first_pass(): jnp.sum(jnp.where(key_mask, jnp.exp(scores - row_top[:, None]), 0.0), axi...  9.7 us
    dot_general x2, matrix products, first_pass(): jnp.einsum('qd,kd->qk', block_rows, key_image, preferred_element_type=jnp...  7.9 us
    all_to_all x1, starting transfers between devices, in_one_piece(): lax.all_to_all(both, axis, split_axis=split_dim, concat_axis=concat_dim,...  7.87 us
    all_to_all x1, waiting for transfers between devices, paired_blocks(): lax.all_to_all(to_owner(row_out), TILE, split_axis=0, concat_axis=0, tile...  7.06 us
    all_to_all x1, waiting for transfers between devices, exchange_in_order(): out = lax.all_to_all(out, axes[k], k, k, tiled=True)  6.28 us
  transfers between devices with their start and end apart: 5, of which 5 were waited for; matrix products, arithmetic and copies ran while one was open for 3% of the time, Pallas kernels for 0%

commit v1 on v0

--- a/solution.py
+++ b/solution.py
@@ -1,13 +1,24 @@
+import functools
 import math
 import jax
 import jax.numpy as jnp
 from jax import lax
 from jax.sharding import Mesh
 from jax.sharding import PartitionSpec as P
+from jax.lax import all_to_all, axis_size
 
 QBLK = 4
 TILE = ("tile_0", "tile_1", "tile_2")
 NEGATIVE = -1e30
+
+
+def place_object(w_in, lane_axis):
+    v1 = tuple((w_in for _ in range(axis_size(lane_axis))))
+    everything = jnp.concatenate(v1, axis=0)
+    return all_to_all(everything, axis_name=lane_axis, split_axis=0, concat_axis=0, tiled=True)
+
+
+_drive_side = functools.partial(place_object, lane_axis="grp")
 
 
 def in_one_piece(arrays, axis, split_dim, concat_dim, along):
@@ -194,7 +205,7 @@
 
 def local(descriptors, pairs, counts):
     score_scale = 2.0 / math.sqrt(descriptors.shape[2])
-    image_rows = lax.all_gather(descriptors, "grp", axis=0, tiled=True)
+    image_rows = _drive_side(descriptors)
     image_ids = lax.iota(jnp.int32, counts.shape[0])
     first_image = pairs[:, 0]
     second = pairs[:, 1]

time: 199 us -> 192 us (0.965)
  between operations: 14.3 us -> 0.93 us
  starting transfers between devices: 20.5 us -> 27.5 us
  waiting for transfers between devices: 103 us -> 98.8 us
  other arithmetic: 20.3 us -> 23.7 us
    all_gather x1 -> x0, waiting for transfers between devices: 52.2 us -> none  [local(): image_rows = lax.all_gather(descriptors, 'grp', axis=0, tiled=True)]
    all_to_all x0 -> x1, waiting for transfers between devices: none -> 48.7 us  [place_object(): all_to_all(everything, axis_name=lane_axis, split_axis=0, concat_axis=0,...]
    all_to_all x0 -> x1, starting transfers between devices: none -> 4.99 us  [place_object(): all_to_all(everything, axis_name=lane_axis, split_axis=0, concat_axis=0,...]
    concatenate x0 -> x1, other arithmetic: none -> 4.19 us  [place_object(): everything = jnp.concatenate(v1, axis=0)]
    all_to_all x1, starting transfers between devices: 7.87 us -> 9.97 us  [in_one_piece(): lax.all_to_all(both, axis, split_axis=split_dim, concat_axis=concat_dim,...]
  transfers between devices with their start and end apart: 5 -> 5, of which waited for: 5 -> 5; matrix products, arithmetic and copies ran while one was open for 3% -> 2% of each run, Pallas kernels for 0% -> 0%
where the time goes in v1:
time: 192 us; the launch traced here: 191 us
  waiting for transfers between devices  98.8 us (51%)
  starting transfers between devices  27.5 us (14%)
  other arithmetic  23.7 us (12%)
  blocking collectives  14.8 us (8%)
  matrix products  13.7 us (7%)
  local copies, waits for them, and re-layouts  11.6 us (6%)
    all_to_all x1, waiting for transfers between devices, place_object(): all_to_all(everything, axis_name=lane_axis, split_axis=0, concat_axis=0,...  48.7 us
    all_to_all x1, waiting for transfers between devices, in_one_piece(): lax.all_to_all(both, axis, split_axis=split_dim, concat_axis=concat_dim,...  32.2 us
    all_to_all x1, blocking collectives, in_one_piece(): lax.all_to_all(both, axis, split_axis=split_dim, concat_axis=concat_dim,...  11 us
    all_to_all x1, starting transfers between devices, in_one_piece(): lax.all_to_all(both, axis, split_axis=split_dim, concat_axis=concat_dim,...  9.97 us
    reduce_sum x2, other arithmetic, first_pass(): jnp.sum(jnp.where(key_mask, jnp.exp(scores - row_top[:, None]), 0.0), axi...  9.69 us
    dot_general x2, matrix products, first_pass(): jnp.einsum('qd,kd->qk', block_rows, key_image, preferred_element_type=jnp...  7.69 us
    all_to_all x1, waiting for transfers between devices, paired_blocks(): lax.all_to_all(to_owner(row_out), TILE, split_axis=0, concat_axis=0, tile...  7.06 us
    all_to_all x1, waiting for transfers between devices, exchange_in_order(): out = lax.all_to_all(out, axes[k], k, k, tiled=True)  6.28 us
  transfers between devices with their start and end apart: 5, of which 5 were waited for; matrix products, arithmetic and copies ran while one was open for 2% of the time, Pallas kernels for 0%

profile of v1, /device:TPU:1, one launch (start us, length us, event | category | flops | bytes accessed | tf_op | source)
XLA Modules:
  0.0 191.2 jit_solution(2028028431227697145)
XLA Ops:
  0.6 4.2 %pad_maximum_fusion = bf16[64,128,256]{2,1,0:T(8,128)(2,1)} fusion(bf16[16,128,256]{2,1,0:T(8,128)(2,1)} %param.9), kind=kLoop, calls=%fused_computation.24 | loop fusion | flops 6291456 | bytes 5242880 | tf_op jit(solution)/shard_map/concatenate | solution.py:17
  4.8 0.0 copy-start
  4.8 5.0 %all-to-all-start = ((bf16[64,128,256]{2,1,0:T(8,128)(2,1)}), bf16[64,128,256]{2,1,0:T(8,128)(2,1)}, u32[]{:S(2)}, u32[]{:S(2)}) async-start(bf16[64,128,256]{2,1,0:T(8,128)(2,1)} %pad_maximum_fusion), calls=%async_computation | async-start | bytes 8388608 | tf_op jit(solution)/shard_map/all_to_all | solution.py:18
  9.8 0.0 copy-done
  9.9 48.7 %all-to-all-done = bf16[64,128,256]{2,1,0:T(8,128)(2,1)} async-done(((bf16[64,128,256]{2,1,0:T(8,128)(2,1)}), bf16[64,128,256]{2,1,0:T(8,128)(2,1)}, u32[]{:S(2)}, u32[]{:S(2)}) %all-to-all-start) | async-done | bytes 4194336 | tf_op jit(solution)/shard_map/all_to_all | solution.py:18
  58.6 2.8 %gather_fusion = bf16[8,128,256]{2,1,0:T(8,128)(2,1)S(1)} fusion(bf16[64,128,256]{2,1,0:T(8,128)(2,1)} %all-to-all-done, s32[1024]{0:T(1024)S(1)} %pad_clamp_fusion.1), kind=kCustom, calls=%fused_computation.clone | custom fusion | bytes 1048608 | tf_op jit(solution)/shard_map/jit(_take)/gather | solution.py:218
  61.4 2.8 %gather_fusion.1 = bf16[8,128,256]{2,1,0:T(8,128)(2,1)S(1)} fusion(bf16[64,128,256]{2,1,0:T(8,128)(2,1)} %all-to-all-done, s32[1024]{0:T(1024)S(1)} %pad_clamp_fusion), kind=kCustom, calls=%fused_computation.1.clone | custom fusion | bytes 1048608 | tf_op jit(solution)/shard_map/jit(_take)/gather | solution.py:219
  64.1 0.2 broadcast_select_fusion
  64.3 0.2 broadcast_in_dim.140
  64.5 0.0 copy-start.1
  64.6 1.7 pad_maximum_fusion.1
  66.3 10.0 %all-to-all-start.1 = ((bf16[32,1,160,256]{3,2,1,0:T(8,128)(2,1)}), bf16[32,1,160,256]{3,2,1,0:T(8,128)(2,1)S(1)}, u32[]{:S(2)}, u32[]{:S(2)}) async-start(bf16[32,1,160,256]{3,2,1,0:T(8,128)(2,1)} %pad_maximum_fusion.1), calls=%async_computation.1 | async-start | bytes 5242880 | tf_op jit(solution)/shard_map/all_to_all | solution.py:27
  76.3 0.0 copy-done.1
  76.3 0.2 select_reduce_fusion.5
  76.5 0.6 dynamic_slice.52
  77.1 0.6 dynamic_slice.53
  77.7 0.1 add.159
  77.8 0.1 add.160
  77.9 0.1 add.162
  78.0 32.2 %all-to-all-done.1 = bf16[32,1,160,256]{3,2,1,0:T(8,128)(2,1)S(1)} async-done(((bf16[32,1,160,256]{3,2,1,0:T(8,128)(2,1)}), bf16[32,1,160,256]{3,2,1,0:T(8,128)(2,1)S(1)}, u32[]{:S(2)}, u32[]{:S(2)}) %all-to-all-start.1) | async-done | bytes 2621472 | tf_op jit(solution)/shard_map/all_to_all | solution.py:27
  110.2 1.5 slice.61
  111.7 20.4 %while.48 = (s32[]{:T(128)}, f32[4096]{0:T(1024)S(1)}, f32[4096]{0:T(1024)S(1)}, f32[2,512]{1,0:T(2,128)S(1)}, s32[2,512]{1,0:T(2,128)S(1)}, /*index=5*/s32[]{:T...) while((s32[]{:T(128)}, f32[4096]{0:T(1024)S(1)}, ...), condition=%wide.region_7.9_spmd.clone, body=%wide.region_2.8_spmd.clone.sunk | while | flops 1098936320 | bytes 19316360 | solution.py:97
  111.8 0.7 compare_reduce_fusion.8
  112.4 0.7 compare_reduce_fusion.7
  113.1 3.8 %select_reduce_fusion.11 = (f32[512]{0:T(512)S(1)}, f32[4096]{0:T(1024)S(1)}, f32[512,4096]{1,0:T(8,128)S(1)}) fusion(pred[4096]{0:T(1024)(128)(4,1)S(1)} %compare_reduce_fusion.7, pred[512]{0:T(512)(128)(4,1)S(1)} %compare_reduce_fusion.8, bf16[4096,256]{1,0:T(8,128)(2,1)} %get-tuple-element.457, bf16[2,512,256]{2,1,0:T(8,128)(2,1)S(1)} %get-tuple-element.456, ...), kind=kOutput, calls=%fused_computation.11.clone.1 | convolution fusion | flops 1084222976 | bytes 10770948 | tf_op jit(solution)/shard_map/while/body/eval_jaxpr/while/body/eval_jaxpr/qd,kd->qk/dot_general | solution.py:83
  117.0 4.8 %select_reduce_fusion.12 = (f32[512]{0:T(512)S(1)}, f32[4096]{0:T(1024)S(1)}) fusion(f32[512,4096]{1,0:T(8,128)S(1)} %get-tuple-element.421, f32[512]{0:T(512)S(1)} %get-tuple-element.422, pred[4096]{0:T(1024)(128)(4,1)S(1)} %compare_reduce_fusion.7, f32[4096]{0:T(1024)S(1)} %get-tuple-element.423, pred[512]{0:T(512)(128)(4,1)S(1)} %compare_reduce_fusion.8), kind=kLoop, calls=%fused_computation.10.clone.1 | loop fusion | flops 14675456 | bytes 8430080 | tf_op jit(solution)/shard_map/while/body/eval_jaxpr/while/body/eval_jaxpr/reduce_sum | solution.py:88
  121.9 0.7 compare_reduce_fusion.8
  122.6 0.7 compare_reduce_fusion.7
  123.3 3.8 %select_reduce_fusion.11 = (f32[512]{0:T(512)S(1)}, f32[4096]{0:T(1024)S(1)}, f32[512,4096]{1,0:T(8,128)S(1)}) fusion(pred[4096]{0:T(1024)(128)(4,1)S(1)} %compare_reduce_fusion.7, pred[512]{0:T(512)(128)(4,1)S(1)} %compare_reduce_fusion.8, bf16[4096,256]{1,0:T(8,128)(2,1)} %get-tuple-element.457, bf16[2,512,256]{2,1,0:T(8,128)(2,1)S(1)} %get-tuple-element.456, ...), kind=kOutput, calls=%fused_computation.11.clone.1 | convolution fusion | flops 1084222976 | bytes 10770948 | tf_op jit(solution)/shard_map/while/body/eval_jaxpr/while/body/eval_jaxpr/qd,kd->qk/dot_general | solution.py:83
  127.2 4.8 %select_reduce_fusion.12 = (f32[512]{0:T(512)S(1)}, f32[4096]{0:T(1024)S(1)}) fusion(f32[512,4096]{1,0:T(8,128)S(1)} %get-tuple-element.421, f32[512]{0:T(512)S(1)} %get-tuple-element.422, pred[4096]{0:T(1024)(128)(4,1)S(1)} %compare_reduce_fusion.7, f32[4096]{0:T(1024)S(1)} %get-tuple-element.423, pred[512]{0:T(512)(128)(4,1)S(1)} %compare_reduce_fusion.8), kind=kLoop, calls=%fused_computation.10.clone.1 | loop fusion | flops 14675456 | bytes 8430080 | tf_op jit(solution)/shard_map/while/body/eval_jaxpr/while/body/eval_jaxpr/reduce_sum | solution.py:88
  132.2 11.0 %all_to_all.35 = f32[32,2,128]{2,1,0:T(2,128)S(1)} all-to-all(f32[32,2,128]{2,1,0:T(2,128)S(1)} %pad_maximum_fusion.2), channel_id=1, replica_groups=mesh['grp'=4,'tile_0'=4,'tile_1'=4,'tile_2'=2] {'tile_0','tile_1','tile_2'}, dimensions={0} | all-to-all | bytes 65536 | tf_op jit(solution)/shard_map/all_to_all | solution.py:27
  143.3 3.8 %all_to_all.36 = f32[16,2,1,1,128]{4,3,2,0,1:T(1,128)S(1)} all-to-all(f32[16,2,1,1,128]{4,3,2,0,1:T(1,128)S(1)} %broadcast_in_dim.147), channel_id=1, replica_groups=mesh['grp'=4,'tile_0'=4,'tile_1'=4,'tile_2'=2] {'tile_2'}, dimensions={1} | all-to-all | bytes 32768 | tf_op jit(solution)/shard_map/all_to_all | solution.py:53
  147.1 0.6 copy.102
  147.7 3.5 %all-to-all-start.5 = ((f32[16,2,1,1,128]{4,3,2,1,0:T(1,128)}), f32[16,2,1,1,128]{4,3,2,1,0:T(1,128)S(1)}, u32[]{:S(2)}, u32[]{:S(2)}) async-start(f32[16,2,1,1,128]{4,3,2,1,0:T(1,128)} %copy.102), calls=%async_computation.5 | async-start | bytes 32768 | tf_op jit(solution)/shard_map/all_to_all | solution.py:53
  151.2 0.1 squeeze.81
  151.3 6.3 %all-to-all-done.5 = f32[16,2,1,1,128]{4,3,2,1,0:T(1,128)S(1)} async-done(((f32[16,2,1,1,128]{4,3,2,1,0:T(1,128)}), f32[16,2,1,1,128]{4,3,2,1,0:T(1,128)S(1)}, u32[]{:S(2)}, u32[]{:S(2)}) %all-to-all-start.5) | async-done | bytes 16416 | tf_op jit(solution)/shard_map/all_to_all | solution.py:53
  157.6 7.6 %while.47 = (s32[]{:T(128)}, f32[2,512]{1,0:T(2,128)S(1)}, bf16[2,512,256]{2,1,0:T(8,128)(2,1)S(1)}, bf16[4096,256]{1,0:T(8,128)(2,1)}, f32[4096]{0:T(1024)S(1)}...) while((s32[]{:T(128)}, f32[2,512]{1,0:T(2,128)S(1)}, ...), condition=%wide.region_10.12_spmd.clone, body=%wide.region_8.11_spmd.clone.sunk | while | flops 1082134528 | bytes 2396269 | solution.py:124
  157.6 0.7 compare_reduce_fusion.6
  158.3 3.0 %select_reduce_fusion.10 = f32[512]{0:T(512)S(1)} fusion(bf16[4096,256]{1,0:T(8,128)(2,1)} %get-tuple-element.482, f32[4096]{0:T(1024)S(1)} %get-tuple-element.483, pred[4096]{0:T(1024)(128)(4,1)S(1)} %compare_reduce_fusion.6, bf16[2,512,256]{2,1,0:T(8,128)(2,1)S(1)} %get-tuple-element.481, s32[]{:T(128)} %get-tuple-element.470), kind=kOutput, calls=%fused_computation.4.clone.1 | convolution fusion | flops 1082129920 | bytes 2381828 | tf_op jit(solution)/shard_map/while/body/eval_jaxpr/while/body/eval_jaxpr/qd,kd->qk/dot_general | solution.py:115
  161.4 0.7 compare_reduce_fusion.6
  162.1 3.0 %select_reduce_fusion.10 = f32[512]{0:T(512)S(1)} fusion(bf16[4096,256]{1,0:T(8,128)(2,1)} %get-tuple-element.482, f32[4096]{0:T(1024)S(1)} %get-tuple-element.483, pred[4096]{0:T(1024)(128)(4,1)S(1)} %compare_reduce_fusion.6, bf16[2,512,256]{2,1,0:T(8,128)(2,1)S(1)} %get-tuple-element.481, s32[]{:T(128)} %get-tuple-element.470), kind=kOutput, calls=%fused_computation.4.clone.1 | convolution fusion | flops 1082129920 | bytes 2381828 | tf_op jit(solution)/shard_map/while/body/eval_jaxpr/while/body/eval_jaxpr/qd,kd->qk/dot_general | solution.py:115
  165.2 0.1 reshape.246
  165.3 1.4 compare_select_fusion
  166.6 4.9 %all-to-all-start.2 = ((f32[32,1,32]{2,1,0:T(1,128)}), f32[32,1,32]{2,1,0:T(1,128)S(1)}, u32[]{:S(2)}, u32[]{:S(2)}) async-start(f32[32,1,32]{2,1,0:T(1,128)} %get-tuple-element.313), calls=%async_computation.2 | async-start | bytes 32768 | tf_op jit(solution)/shard_map/all_to_all | solution.py:191
  171.6 7.1 %all-to-all-done.2 = f32[32,1,32]{2,1,0:T(1,128)S(1)} async-done(((f32[32,1,32]{2,1,0:T(1,128)}), f32[32,1,32]{2,1,0:T(1,128)S(1)}, u32[]{:S(2)}, u32[]{:S(2)}) %all-to-all-start.2) | async-done | bytes 4128 | tf_op jit(solution)/shard_map/all_to_all | solution.py:191
  178.6 4.2 %all-to-all-start.6 = ((f32[32,1,32]{2,1,0:T(1,128)}), f32[32,1,32]{2,1,0:T(1,128)S(1)}, u32[]{:S(2)}, u32[]{:S(2)}) async-start(f32[32,1,32]{2,1,0:T(1,128)} %get-tuple-element.312), calls=%async_computation.6 | async-start | bytes 32768 | tf_op jit(solution)/shard_map/all_to_all | solution.py:192
  182.8 0.7 add_select_fusion
  183.4 0.5 broadcast.199
  184.0 0.7 reduce.12
  184.6 0.7 reshape_transpose_reshape.10
  185.3 4.5 %all-to-all-done.6 = f32[32,1,32]{2,1,0:T(1,128)S(1)} async-done(((f32[32,1,32]{2,1,0:T(1,128)}), f32[32,1,32]{2,1,0:T(1,128)S(1)}, u32[]{:S(2)}, u32[]{:S(2)}) %all-to-all-start.6) | async-done | bytes 4128 | tf_op jit(solution)/shard_map/all_to_all | solution.py:192
  189.9 0.7 reduce.13
  190.6 0.7 reshape_transpose_reshape.11
  (31 shorter events, 0.5 us)
Async XLA Ops:
  4.8 5.0 %copy-start = (s32[8,2]{0,1:T(2,128)S(1)}, s32[8,2]{0,1:T(2,128)}, u32[]{:S(2)}) copy-start(s32[8,2]{0,1:T(2,128)} %param.10) | copy-start | bytes 196
  4.8 53.8 %all-to-all-start = ((bf16[64,128,256]{2,1,0:T(8,128)(2,1)}), bf16[64,128,256]{2,1,0:T(8,128)(2,1)}, u32[]{:S(2)}, u32[]{:S(2)}) async-start(bf16[64,128,256]{2,1,0:T(8,128)(2,1)} %pad_maximum_fusion), calls=%async_computation | async-start | bytes 8388608 | tf_op jit(solution)/shard_map/all_to_all | solution.py:18
  64.5 11.8 %copy-start.1 = (s32[64]{0:T(128)S(1)}, s32[64]{0:T(128)}, u32[]{:S(2)}) copy-start(s32[64]{0:T(128)} %param.11) | copy-start | bytes 772
  66.3 43.9 %all-to-all-start.1 = ((bf16[32,1,160,256]{3,2,1,0:T(8,128)(2,1)}), bf16[32,1,160,256]{3,2,1,0:T(8,128)(2,1)S(1)}, u32[]{:S(2)}, u32[]{:S(2)}) async-start(bf16[32,1,160,256]{3,2,1,0:T(8,128)(2,1)} %pad_maximum_fusion.1), calls=%async_computation.1 | async-start | bytes 5242880 | tf_op jit(solution)/shard_map/all_to_all | solution.py:27
  147.7 9.9 %all-to-all-start.5 = ((f32[16,2,1,1,128]{4,3,2,1,0:T(1,128)}), f32[16,2,1,1,128]{4,3,2,1,0:T(1,128)S(1)}, u32[]{:S(2)}, u32[]{:S(2)}) async-start(f32[16,2,1,1,128]{4,3,2,1,0:T(1,128)} %copy.102), calls=%async_computation.5 | async-start | bytes 32768 | tf_op jit(solution)/shard_map/all_to_all | solution.py:53
  166.6 12.0 %all-to-all-start.2 = ((f32[32,1,32]{2,1,0:T(1,128)}), f32[32,1,32]{2,1,0:T(1,128)S(1)}, u32[]{:S(2)}, u32[]{:S(2)}) async-start(f32[32,1,32]{2,1,0:T(1,128)} %get-tuple-element.313), calls=%async_computation.2 | async-start | bytes 32768 | tf_op jit(solution)/shard_map/all_to_all | solution.py:191
  178.6 11.2 %all-to-all-start.6 = ((f32[32,1,32]{2,1,0:T(1,128)}), f32[32,1,32]{2,1,0:T(1,128)S(1)}, u32[]{:S(2)}, u32[]{:S(2)}) async-start(f32[32,1,32]{2,1,0:T(1,128)} %get-tuple-element.312), calls=%async_computation.6 | async-start | bytes 32768 | tf_op jit(solution)/shard_map/all_to_all | solution.py:192
